TPU v7x, 32 devices: a whole 2x2x4 slice. The times are simulated.
32 devices in a mesh: energy: 8 (over y, x, core), cell: 4 (over z).
Axes of the slice: x: 2, y: 2, z: 4, core: 2. Of those that a mesh axis runs over, the one named last changes fastest.
Arguments:
- g_retarded: bfloat16 [2, 8, 4, 128, 512], P(None, 'energy', None, None, 'cell'), may hold values from -0.75 to 0.75
- sigma_lesser: bfloat16 [2, 8, 128, 512], P(None, 'energy', None, 'cell'), may hold values from -1.5 to 1.5
- w_screened: bfloat16 [2, 8, 4, 128, 512], P(None, 'energy', None, None, 'cell'), may hold values from -0.75 to 0.75
- coupling: int32 [4, 4], replicated, may hold values 0 or 1
Outputs:
- polarization: bfloat16 [4, 2, 8, 16384], P('cell', None, 'energy')
- w_lesser: bfloat16 [4, 2, 8, 128, 128], P('cell', None, 'energy')
Inputs may be any that keep to these rules, and one draw needn't show every extreme that they name: coupling[i, j] is 1 where cell i is coupled to cell j and 0 elsewhere.
All inputs are finite; a program needn't handle non-finite values.
Results may differ from a plain program's by a relative error of at most 0.024.
Values may be sent and summed in bfloat16 or wider, within the bound.
No kernel may reach another device: no remote copies, remote signals or barrier semaphores. Data moves between devices by JAX's collectives and lax.ppermute only.
A program may use at most 64 MiB of HBM per device.

v0:
```python
import math
import jax
import jax.numpy as jnp
from jax import lax
from jax.sharding import PartitionSpec as P


def forward_product(left, right):
    return jnp.einsum("eibjc,ecjd->eibjd", left, right, preferred_element_type=jnp.float32)


def adjoint_product(left, right):
    return jnp.einsum("eibjc,eidjc->iebd", left, right, preferred_element_type=jnp.float32)


def sandwich_rows(columns, sources, coupling, cell_index, count):
    orbitals = sources.shape[2]
    local_cells = sources.shape[3] // orbitals
    energies = sources.shape[1]
    rows_block = columns
    rows_block = rows_block.reshape(2, energies, count, orbitals, local_cells, orbitals)
    col_re = rows_block[0]
    col_im = rows_block[1]
    source = sources.reshape(2, energies, orbitals, local_cells, orbitals)
    src_re = source[0]
    src_im = source[1]
    mid_re = (forward_product(col_re, src_re) - forward_product(col_im, src_im)).astype(
        jnp.bfloat16
    )
    mid_im = (forward_product(col_re, src_im) + forward_product(col_im, src_re)).astype(
        jnp.bfloat16
    )
    weight = lax.dynamic_slice(coupling, (0, cell_index * local_cells), (count, local_cells))
    weight = weight.astype(jnp.bfloat16)[None, :, None, :, None]
    mid_re = mid_re * weight
    mid_im = mid_im * weight
    part_re = adjoint_product(mid_re, col_re) + adjoint_product(mid_im, col_im)
    part_im = adjoint_product(mid_im, col_re) - adjoint_product(mid_re, col_im)
    return jnp.stack([part_re, part_im], axis=1)


def correlate_spectral(spread):
    energies = spread.shape[2]
    length = 2 * energies
    freqs = jnp.arange(length, dtype=jnp.int32)[:, None]
    points = jnp.arange(energies, dtype=jnp.int32)[None, :]
    phase = jnp.mod(freqs * points, length).astype(jnp.float32) * (math.pi / energies)
    cos_table = jnp.cos(phase)
    sin_table = jnp.sin(phase)
    cos_high = cos_table.astype(jnp.bfloat16)
    cos_low = (cos_table - cos_high.astype(jnp.float32)).astype(jnp.bfloat16)
    sin_high = sin_table.astype(jnp.bfloat16)
    sin_low = (sin_table - sin_high.astype(jnp.float32)).astype(jnp.bfloat16)

    def forward(high, low, data):
        upper = jnp.einsum("ft,ctk->cfk", high, data, preferred_element_type=jnp.float32)
        return upper + jnp.einsum("ft,ctk->cfk", low, data, preferred_element_type=jnp.float32)

    def inverse(table, data):
        return jnp.einsum("ft,cfk->ctk", table, data, precision=lax.Precision.HIGH)

    low_re = spread[:, 0]
    low_im = spread[:, 1]
    high_re = spread[:, 2]
    high_im = spread[:, 3]
    spec_a_re = forward(cos_high, cos_low, low_re) + forward(sin_high, sin_low, low_im)
    spec_a_im = forward(cos_high, cos_low, low_im) - forward(sin_high, sin_low, low_re)
    spec_b_re = forward(cos_high, cos_low, high_re) + forward(sin_high, sin_low, high_im)
    spec_b_im = forward(cos_high, cos_low, high_im) - forward(sin_high, sin_low, high_re)
    cross_re = spec_a_re * spec_b_re + spec_a_im * spec_b_im
    cross_im = spec_a_im * spec_b_re - spec_a_re * spec_b_im
    back_re = (inverse(cos_table, cross_re) - inverse(sin_table, cross_im)) / length
    back_im = (inverse(cos_table, cross_im) + inverse(sin_table, cross_re)) / length
    factor = 1.0 / math.sqrt(energies)
    return jnp.stack([back_im * factor, -back_re * factor], axis=1)


def on_device(g_retarded, sigma_lesser, w_screened, coupling):
    cell_index = lax.axis_index("cell")
    orbitals = sigma_lesser.shape[2]
    local_cells = sigma_lesser.shape[3] // orbitals
    energies_dev = sigma_lesser.shape[1]
    lesser = lax.psum_scatter(
        sandwich_rows(
            g_retarded, sigma_lesser, coupling, cell_index, local_cells * lax.axis_size("cell")
        ).astype(jnp.bfloat16),
        "cell",
        scatter_dimension=0,
        tiled=True,
    ).astype(jnp.float32)
    row_block = lax.dynamic_slice_in_dim(g_retarded, cell_index * local_cells + 0, 1, 2)
    blocks = [row_block[:, :, 0, :, 0:orbitals]]
    diagonal = jnp.stack(blocks, axis=0).astype(jnp.float32)
    diag_re = diagonal[:, 0]
    diag_im = diagonal[:, 1]
    greater = lesser + jnp.stack(
        [diag_re - jnp.swapaxes(diag_re, -1, -2), diag_im + jnp.swapaxes(diag_im, -1, -2)], axis=1
    )
    both = jnp.concatenate([lesser, greater], axis=1).astype(jnp.bfloat16)
    flat = both.reshape(local_cells, 4, energies_dev, orbitals * orbitals)
    spread = lax.all_to_all(flat, "energy", split_axis=3, concat_axis=2, tiled=True)
    polar = correlate_spectral(spread).astype(jnp.bfloat16)
    polar_local = lax.all_to_all(polar, "energy", split_axis=2, concat_axis=3, tiled=True)
    sources = polar_local.reshape(local_cells, 2, energies_dev, orbitals, orbitals)
    sources = jnp.transpose(sources, (1, 2, 3, 0, 4)).reshape(
        2, energies_dev, orbitals, local_cells * orbitals
    )
    screened = lax.psum_scatter(
        sandwich_rows(
            w_screened, sources, coupling, cell_index, local_cells * lax.axis_size("cell")
        ).astype(jnp.bfloat16),
        "cell",
        scatter_dimension=0,
        tiled=True,
    )
    return (polar_local, screened)


def solution(mesh):
    return jax.shard_map(
        on_device,
        mesh=mesh,
        in_specs=(
            P(None, "energy", None, None, "cell"),
            P(None, "energy", None, "cell"),
            P(None, "energy", None, None, "cell"),
            P(),
        ),
        out_specs=(P("cell", None, "energy", None), P("cell", None, "energy", None, None)),
        check_vma=False,
    )
```

profile of v0, /device:TPU:0, one launch (start us, length us, event | category | flops | bytes accessed | tf_op | source)
XLA Modules:
  0.0 264.8 jit_solution(17689031934140179815)
XLA Ops:
  7.2 1.1 fusion.61
  8.3 1.1 fusion.65
  9.5 0.9 fusion.127
  10.4 1.1 fusion.31
  11.5 1.1 fusion.59
  12.6 1.1 fusion.29
  13.8 1.1 fusion.63
  14.9 1.1 fusion.24
  16.1 1.1 fusion.25
  17.2 0.7 pad_maximum_fusion
  18.0 0.9 constant_dynamic-slice_fusion.1
  19.4 1.2 dynamic-slice
  20.6 35.8 %all-reduce.5.cloned.1.call-done = bf16[4,2,1,128,128]{4,3,0,2,1:T(8,128)(2,1)} async-done(((bf16[4,2,1,128,128]{4,3,0,2,1:T(8,128)(2,1)}), bf16[4,2,1,128,128]{4,3,0,2,1:T(8,128)(2,1)}) %all-reduce.5.cloned.1.call-update) | async-done | bytes 262160
  56.4 1.5 fusion.36
  58.2 12.9 %copy.76 = bf16[1,4,1,16384]{1,2,0,3:T(2,128)(2,1)} copy(bf16[1,4,1,16384]{3,1,2,0:T(4,128)(2,1)S(1)} %pad_maximum_fusion.2) | data formatting | bytes 262144 | tf_op jit(solution)/shard_map/concatenate | solution.py:99
  71.0 0.5 broadcast.79
  71.6 90.8 %reduce.6 = bf16[16384,4]{1,0:T(8,128)(2,1)} reduce(bf16[16384,1,1,4]{3,2,1,0:T(2,128)(2,1)} %bitcast.233, bf16[]{:T(256)} %broadcast.79), dimensions={1,2}, to_apply=%bitcast.220.reduce_sub_computation | reduce | bytes 262146
  162.3 8.7 %reshape.445 = bf16[8,2,4096]{2,1,0:T(2,128)(2,1)S(1)} reshape(bf16[16384,4]{1,0:T(8,128)(2,1)} %reduce.6) | data formatting | bytes 262144
  171.0 9.0 %all_to_all.24 = bf16[8,2,4096]{2,1,0:T(2,128)(2,1)S(1)} all-to-all(bf16[8,2,4096]{2,1,0:T(2,128)(2,1)S(1)} %reshape.445), channel_id=1, replica_groups=mesh['energy'=8,'cell'=4] {'energy'}, dimensions={0} | all-to-all | bytes 262144 | tf_op jit(solution)/shard_map/all_to_all | solution.py:101
  180.0 11.1 %reshape.446 = bf16[16384,1,1,4]{3,2,1,0:T(2,128)(2,1)} reshape(bf16[8,2,4096]{2,1,0:T(2,128)(2,1)S(1)} %all_to_all.24) | data formatting | bytes 262144
  191.1 15.4 %copy.77 = bf16[1,4,1,16384]{3,1,2,0:T(4,128)(2,1)S(1)} copy(bf16[1,4,1,16384]{1,2,0,3:T(2,128)(2,1)} %bitcast.234) | data formatting | bytes 262144 | tf_op jit(solution)/shard_map/all_to_all | solution.py:101
  209.8 0.3 fusion.50
  210.1 0.3 fusion.52
  210.4 0.3 fusion.11
  210.7 0.3 fusion.10
  211.0 7.4 %all_to_all.25 = bf16[1,2,8,2048]{3,1,0,2:T(2,128)(2,1)S(1)} all-to-all(bf16[1,2,8,2048]{3,1,0,2:T(2,128)(2,1)S(1)} %copy.78), channel_id=1, replica_groups=mesh['energy'=8,'cell'=4] {'energy'}, dimensions={2} | all-to-all | bytes 131072 | tf_op jit(solution)/shard_map/all_to_all | solution.py:103
  218.4 0.3 slice_reduce_fusion.1
  220.1 0.2 fusion.21
  220.6 0.7 pad_maximum_fusion.1
  221.4 33.8 %all-reduce.7.cloned.1.call-done = bf16[4,2,1,128,128]{4,3,0,2,1:T(8,128)(2,1)} async-done(((bf16[4,2,1,128,128]{4,3,0,2,1:T(8,128)(2,1)}), bf16[4,2,1,128,128]{4,3,0,2,1:T(8,128)(2,1)}) %all-reduce.7.cloned.1.call-update) | async-done | bytes 262160
  255.2 2.1 dynamic-slice_bitcast_fusion
  257.3 0.6 copy.117
  (45 shorter events, 5.7 us)
Async XLA Ops:
  7.2 49.3 %all-reduce.5.cloned.1.call-start = ((), (), s32[]{:S(2)}) async-start(), calls=%async_computation.2 | async-start | bytes 524288
  18.0 237.2 %all-reduce.7.cloned.1.call-start = ((), (), s32[]{:S(2)}) async-start(), calls=%async_computation.3 | async-start | bytes 524288
  191.1 27.7 %copy-start = (bf16[2,1,4,128,128]{4,3,2,1,0:T(8,128)(2,1)S(1)}, bf16[2,1,4,128,128]{4,3,2,1,0:T(8,128)(2,1)}, u32[]{:S(2)}) copy-start(bf16[2,1,4,128,128]{4,3,2,1,0:T(8,128)(2,1)} %param.6) | copy-start | bytes 786436
Sparse Core Ops, SparseCore 0:
  18.1 38.2 all-reduce.4
  221.5 33.6 all-reduce.6
where the time goes:
time: 266 us; the launch traced here: 265 us
  other arithmetic  94.8 us (36%)
  waiting for transfers between devices  69.6 us (26%)
  local copies, waits for them, and re-layouts  54.4 us (20%)
  blocking collectives  16.4 us (6%)
  matrix products  15.2 us (6%)
  between operations  14.4 us (5%)
    unnamed x1, other arithmetic  90.8 us
    unnamed x4, waiting for transfers between devices  69.6 us
    unnamed x10, local copies, waits for them, and re-layouts  24.5 us
    all_to_all x1, local copies, waits for them, and re-layouts, on_device(): lax.all_to_all(flat, 'energy', split_axis=3, concat_axis=2, tiled=True)  15.4 us
    concatenate x3, local copies, waits for them, and re-layouts, on_device(): both = jnp.concatenate([lesser, greater], axis=1).astype(jnp.bfloat16)  12.9 us
    all_to_all x1, blocking collectives, on_device(): lax.all_to_all(flat, 'energy', split_axis=3, concat_axis=2, tiled=True)  8.95 us
    all_to_all x1, blocking collectives, on_device(): lax.all_to_all(polar, 'energy', split_axis=2, concat_axis=3, tiled=True)  7.4 us
    dot_general x8, matrix products, adjoint_product(): jnp.einsum('eibjc,eidjc->iebd', left, right, preferred_element_type=jnp.f...  5.52 us
  transfers between devices with their start and end apart: 2, of which 2 were waited for; matrix products, arithmetic and copies ran while one was open for 1% of the time, Pallas kernels for 0%

commit v1 on v0

--- a/solution.py
+++ b/solution.py
@@ -98,7 +98,10 @@
     )
     both = jnp.concatenate([lesser, greater], axis=1).astype(jnp.bfloat16)
     flat = both.reshape(local_cells, 4, energies_dev, orbitals * orbitals)
-    spread = lax.all_to_all(flat, "energy", split_axis=3, concat_axis=2, tiled=True)
+    spread = jnp.concatenate(
+        lax.all_to_all(jnp.stack(jnp.split(flat, lax.axis_size("energy"), axis=3)), "energy", 0, 0),
+        axis=2,
+    )
     polar = correlate_spectral(spread).astype(jnp.bfloat16)
     polar_local = lax.all_to_all(polar, "energy", split_axis=2, concat_axis=3, tiled=True)
     sources = polar_local.reshape(local_cells, 2, energies_dev, orbitals, orbitals)

time: 266 us -> 120 us (0.45)
  other arithmetic: 94.8 us -> 3.43 us
  local copies, waits for them, and re-layouts: 54.4 us -> 5.83 us
  matrix products: 15.2 us -> 8.77 us
    unnamed x1 -> x7, other arithmetic: 90.8 us -> 0.22 us
    unnamed x10 -> x18, local copies, waits for them, and re-layouts: 24.5 us -> 4.9 us
    all_to_all x1 -> x0, local copies, waits for them, and re-layouts: 15.4 us -> none  [on_device(): lax.all_to_all(flat, 'energy', split_axis=3, concat_axis=2, tiled=True)]
    concatenate x3 -> x2, local copies, waits for them, and re-layouts: 12.9 us -> 0.04 us  [on_device(): both = jnp.concatenate([lesser, greater], axis=1).astype(jnp.bfloat16)]
    dot_general x8, matrix products: 5.52 us -> 1.9 us  [adjoint_product(): jnp.einsum('eibjc,eidjc->iebd', left, right, preferred_element_type=jnp.f...]
    dot_general x8, matrix products: 5.35 us -> 2.62 us  [forward_product(): jnp.einsum('eibjc,ecjd->eibjd', left, right, preferred_element_type=jnp.f...]
where the time goes in v1:
time: 120 us
  waiting for transfers between devices  70.5 us (59%)
  blocking collectives  16.5 us (14%)
  between operations  14.4 us (12%)
  matrix products  8.77 us (7%)
  local copies, waits for them, and re-layouts  5.83 us (5%)
  other arithmetic  3.43 us (3%)
    unnamed x4, waiting for transfers between devices  70.5 us
    all_to_all x1, blocking collectives, on_device(): lax.all_to_all(jnp.stack(jnp.split(flat, lax.axis_size('energy'), axis=3)...  8.95 us
    all_to_all x1, blocking collectives, on_device(): lax.all_to_all(polar, 'energy', split_axis=2, concat_axis=3, tiled=True)  7.53 us
    unnamed x18, local copies, waits for them, and re-layouts  4.9 us
    dot_general x8, matrix products, forward_product(): jnp.einsum('eibjc,ecjd->eibjd', left, right, preferred_element_type=jnp.f...  2.62 us
  transfers between devices with their start and end apart: 2, of which 2 were waited for; matrix products, arithmetic and copies ran while one was open for 1% of the time, Pallas kernels for 0%

profile of v1, /device:TPU:0, one launch (start us, length us, event | category | flops | bytes accessed | tf_op | source)
XLA Modules:
  0.0 119.5 jit_solution(8124895543061045879)
XLA Ops:
  7.2 1.2 fusion.61
  8.6 0.7 copy-done.3
  9.5 0.2 fusion.31
  9.7 0.2 fusion.59
  10.0 0.2 fusion.29
  10.2 0.2 fusion.63
  10.4 0.2 fusion.24
  10.7 0.2 fusion.25
  10.9 0.7 pad_maximum_fusion
  12.2 0.6 copy-done.4
  12.9 0.6 dynamic-slice
  13.5 36.7 %all-reduce.5.cloned.1.call-done = bf16[4,2,1,128,128]{4,3,0,2,1:T(8,128)(2,1)} async-done(((bf16[4,2,1,128,128]{4,3,0,2,1:T(8,128)(2,1)}), bf16[4,2,1,128,128]{4,3,0,2,1:T(8,128)(2,1)}) %all-reduce.5.cloned.1.call-update) | async-done | bytes 262160
  50.1 1.5 %fusion.36 = (bf16[1,2,1,128,128]{4,3,0,2,1:T(8,128)(2,1)S(1)}, bf16[1,2,1,128,128]{4,3,0,2,1:T(8,128)(2,1)S(1)}) fusion(f32[1,1,1,128,128]{4,3,0,2,1:T(8,128)S(1)} %fusion.83, f32[1,1,1,128,128]{4,3,0,2,1:T(8,128)S(1)} %copy.95, bf16[4,2,1,128,128]{4,3,0,2,1:T(8,128)(2,1)} %all-reduce.5.cloned.1.call-done, u32[]{:T(128)} %bitcast.83), kind=kLoop, calls=%fused_computation.71 | loop fusion | flops 131072 | bytes 327684 | tf_op jit(solution)/shard_map/convert.14
  52.0 8.9 %all_to_all.17 = bf16[8,1,4,1,2048]{4,2,3,1,0:T(4,128)(2,1)S(1)} all-to-all(bf16[8,1,4,1,2048]{4,2,3,1,0:T(4,128)(2,1)S(1)} %constant_dynamic-update-slice_fusion), channel_id=1, replica_groups=mesh['energy'=8,'cell'=4] {'energy'}, dimensions={0} | all-to-all | bytes 262144 | tf_op jit(solution)/shard_map/all_to_all | solution.py:102
  64.2 0.2 multiply_subtract_fusion
  64.4 0.3 fusion.50
  64.7 0.3 fusion.52
  65.0 0.3 fusion.11
  65.3 0.3 fusion.10
  65.7 7.5 %all_to_all.18 = bf16[1,2,8,2048]{3,1,0,2:T(2,128)(2,1)S(1)} all-to-all(bf16[1,2,8,2048]{3,1,0,2:T(2,128)(2,1)S(1)} %copy.96), channel_id=1, replica_groups=mesh['energy'=8,'cell'=4] {'energy'}, dimensions={2} | all-to-all | bytes 131072 | tf_op jit(solution)/shard_map/all_to_all | solution.py:106
  73.2 0.3 slice_reduce_fusion.1
  73.8 0.2 fusion.43
  74.0 0.2 fusion.33
  74.2 0.2 fusion.45
  74.4 0.2 fusion.35
  74.6 0.2 fusion.41
  74.9 0.2 fusion.21
  75.1 0.2 fusion.20
  75.4 0.7 pad_maximum_fusion.1
  76.1 33.8 %all-reduce.7.cloned.1.call-done = bf16[4,2,1,128,128]{4,3,0,2,1:T(8,128)(2,1)} async-done(((bf16[4,2,1,128,128]{4,3,0,2,1:T(8,128)(2,1)}), bf16[4,2,1,128,128]{4,3,0,2,1:T(8,128)(2,1)}) %all-reduce.7.cloned.1.call-update) | async-done | bytes 262160
  109.9 2.1 %dynamic-slice_bitcast_fusion = bf16[1,2,1,128,128]{4,3,2,1,0:T(8,128)(2,1)} fusion(bf16[4,2,1,128,128]{4,3,0,2,1:T(8,128)(2,1)} %all-reduce.7.cloned.1.call-done, u32[]{:T(128)} %bitcast.83), kind=kLoop, calls=%fused_computation.126 | loop fusion | bytes 131076
  112.1 0.6 copy.143
  (58 shorter events, 4.8 us)
Async XLA Ops:
  7.2 1.2 %copy-start = (bf16[2,1,4,128,128]{4,3,2,1,0:T(8,128)(2,1)S(1)}, bf16[2,1,4,128,128]{4,3,2,1,0:T(8,128)(2,1)}, u32[]{:S(2)}) copy-start(bf16[2,1,4,128,128]{4,3,2,1,0:T(8,128)(2,1)} %param.4) | copy-start | bytes 786436
  7.2 43.0 %all-reduce.5.cloned.1.call-start = ((), (), s32[]{:S(2)}) async-start(), calls=%async_computation.2 | async-start | bytes 524288
  7.2 1.2 copy-start.2
  8.6 0.7 copy-start.3
  11.7 98.3 %all-reduce.7.cloned.1.call-start = ((), (), s32[]{:S(2)}) async-start(), calls=%async_computation.3 | async-start | bytes 524288
  12.2 0.7 copy-start.4
  65.7 7.9 %copy-start.1 = (bf16[2,1,4,128,128]{4,3,2,1,0:T(8,128)(2,1)S(1)}, bf16[2,1,4,128,128]{4,3,2,1,0:T(8,128)(2,1)}, u32[]{:S(2)}) copy-start(bf16[2,1,4,128,128]{4,3,2,1,0:T(8,128)(2,1)} %param.6) | copy-start | bytes 786436
Sparse Core Ops, SparseCore 0:
  11.8 38.3 all-reduce.4
  76.2 33.6 all-reduce.6
